TPU v7x, 32 devices: a whole 2x2x4 slice. The times are simulated.
32 devices in a mesh: seq: 8 (over z, x), head: 4 (over y, core).
Axes of the slice: x: 2, y: 2, z: 4, core: 2. Of those that a mesh axis runs over, the one named last changes fastest.
Arguments:
- tokens: bfloat16 [2048, 3584], P('seq'), may hold values from -16 to 16
- length: int32 [1], replicated, may hold values from 512 to 2048
- in_gain: float32 [3584], replicated, may hold values from 0.5 to 1.5
- q_weight: bfloat16 [3584, 3584], P(None, 'head'), may hold values from -0.09375 to 0.09375
- q_bias: float32 [3584], P('head'), may hold values from -60 to 60
- k_weight: bfloat16 [3584, 512], P(None, 'head'), may hold values from -0.09375 to 0.09375
- k_bias: float32 [512], P('head'), may hold values from -60 to 60
- v_weight: bfloat16 [3584, 512], P(None, 'head'), may hold values from -0.09375 to 0.09375
- v_bias: float32 [512], P('head'), may hold values from -2 to 2
- o_weight: bfloat16 [3584, 3584], P('head'), may hold values from -0.125 to 0.125
- final_gain: float32 [3584], P('head'), may hold values from 0.5 to 1.5
Outputs:
- hidden: bfloat16 [2048, 3584], P('seq', 'head')
- embedding: float32 [3584], P('head')
All inputs are finite; a program needn't handle non-finite values.
Results may differ from a plain program's by a relative error of at most 0.0075.
The roundings to bfloat16 on the way count: a program that leaves them out, or rounds other values in their place, can miss the bound.
Values may be sent and summed in bfloat16 or wider, within the bound.
A program may use at most 192 MiB of HBM per device.

v0:
```python
import jax
import jax.numpy as jnp
from jax import lax
from jax.sharding import PartitionSpec as P

D = 3584
HEAD_DIM = 128
rope_base = 1000000.0
epsilon = 1e-06


def rms_norm(inputs, gain):
    inputs = inputs.astype(jnp.float32)
    return inputs * lax.rsqrt(jnp.mean(inputs * inputs, axis=-1, keepdims=True) + epsilon) * gain


def rope_tables(positions):
    half_dim = HEAD_DIM // 2
    inverse = rope_base ** (-(jnp.arange(half_dim, dtype=jnp.float32) * 2.0) / HEAD_DIM)
    angles = positions.astype(jnp.float32)[:, None] * inverse[None, :]
    angles = jnp.concatenate([angles, angles], axis=1)
    return (jnp.cos(angles), jnp.sin(angles))


def rotate(inputs, cosine, sine):
    half_dim = HEAD_DIM // 2
    turned = jnp.concatenate([-inputs[..., half_dim:], inputs[..., :half_dim]], axis=-1)
    return inputs * cosine[:, None, :] + turned * sine[:, None, :]


def key_scores(queries, key_block):
    return lax.dot_general(
        queries, key_block, (((1,), (1,)), ((), ())), preferred_element_type=jnp.float32
    )


def body(
    tokens,
    length,
    in_gain,
    q_weight,
    q_bias,
    k_weight,
    k_bias,
    v_weight,
    v_bias,
    o_weight,
    final_gain,
):
    tok_rows = tokens.shape[0]
    head_count = q_weight.shape[1] // HEAD_DIM
    offset = lax.axis_index("seq") * tok_rows
    limit = length[0]
    positions = offset + jnp.arange(tok_rows, dtype=jnp.int32)
    normed = rms_norm(tokens, in_gain).astype(jnp.bfloat16)
    cosine, sine = rope_tables(positions)
    query = jnp.dot(normed, q_weight, preferred_element_type=jnp.float32) + q_bias
    query = rotate(query.reshape(tok_rows, head_count, HEAD_DIM), cosine, sine) * HEAD_DIM ** (-0.5)
    query = query.astype(jnp.bfloat16).reshape(tok_rows * head_count, HEAD_DIM)
    keys = jnp.dot(normed, k_weight, preferred_element_type=jnp.float32) + k_bias
    keys = (
        rotate(keys.reshape(tok_rows, 1, HEAD_DIM), cosine, sine)
        .astype(jnp.bfloat16)
        .reshape(tok_rows, HEAD_DIM)
    )
    values = (jnp.dot(normed, v_weight, preferred_element_type=jnp.float32) + v_bias).astype(
        jnp.bfloat16
    )
    q_rows = query.shape[0]

    def absorb(carry, piece):
        top, total, accum = carry
        k_piece, v_piece = piece
        count = k_piece.shape[0]
        live = jnp.arange(count, dtype=jnp.int32) < limit
        scores = jnp.where(live[None, :], key_scores(query, k_piece), -1e30)
        new_top = jnp.maximum(top, jnp.max(scores, axis=1))
        weights = jnp.where(live[None, :], jnp.exp(scores - new_top[:, None]), 0.0)
        total = jnp.sum(weights, axis=1)
        accum = jnp.dot(weights.astype(jnp.bfloat16), v_piece, preferred_element_type=jnp.float32)
        return (new_top, total, accum)

    initial = (
        jnp.full((q_rows,), -1e30, jnp.float32),
        jnp.zeros((q_rows,), jnp.float32),
        jnp.zeros((q_rows, HEAD_DIM), jnp.float32),
    )
    piece = (
        lax.all_gather(keys, "seq", axis=0, tiled=True),
        lax.all_gather(values, "seq", axis=0, tiled=True),
    )

    def update(state):
        return absorb(state, piece)

    def unchanged(state):
        return state

    top, total, accum = lax.cond(jnp.int32(0) < limit, update, unchanged, initial)
    attended = (
        (accum / total[:, None]).astype(jnp.bfloat16).reshape(tok_rows, head_count * HEAD_DIM)
    )
    mixed = jnp.dot(attended, o_weight, preferred_element_type=jnp.float32)
    width_share = D // lax.axis_size("head")
    column = lax.axis_index("head") * width_share
    shared = lax.psum_scatter(
        mixed.astype(jnp.bfloat16), "head", scatter_dimension=1, tiled=True
    ).astype(jnp.float32)
    hidden_full = (
        lax.dynamic_slice_in_dim(tokens, column, width_share, 1).astype(jnp.float32) + shared
    )
    squares = lax.psum(jnp.sum(hidden_full * hidden_full, axis=1), "head")
    final = hidden_full * lax.rsqrt(squares[:, None] / D + epsilon) * final_gain
    row_live = positions < limit
    local_sum = jnp.sum(jnp.where(row_live[:, None], final, 0.0), axis=0)
    pooled_sum = lax.psum(local_sum, "seq")
    mean = pooled_sum / limit.astype(jnp.float32)
    power = lax.psum(jnp.sum(mean * mean), "head")
    embedding = mean * lax.rsqrt(power / D + epsilon)
    return (hidden_full.astype(jnp.bfloat16), embedding)


def solution(mesh):
    in_specs = (
        P("seq", None),
        P(),
        P(),
        P(None, "head"),
        P("head"),
        P(None, "head"),
        P("head"),
        P(None, "head"),
        P("head"),
        P("head", None),
        P("head"),
    )
    out_specs = (P("seq", "head"), P("head"))
    return jax.shard_map(body, mesh=mesh, in_specs=in_specs, out_specs=out_specs, check_vma=False)
```

profile of v0, /device:TPU:0, one launch (start us, length us, event | category | flops | bytes accessed | tf_op | source)
XLA Modules:
  0.0 211.3 jit_solution(12068621012374544557)
XLA Ops:
  7.2 2.0 fusion.7
  9.3 6.5 %convolution_add_fusion = f32[256,896]{1,0:T(8,128)} fusion(bf16[3584,896]{1,0:T(8,128)(2,1)} %param.16, f32[896]{0:T(1024)} %param.17, bf16[256,3584]{1,0:T(8,128)(2,1)} %param.13, f32[3584]{0:T(1024)} %param.15, f32[256]{0:T(256)S(1)} %add_rsqrt_fusion.1), kind=kOutput, calls=%fused_computation.16 | convolution fusion | flops 1648066560 | bytes 9193984 | tf_op jit(solution)/shard_map/dot_general | solution.py:57
  15.7 2.6 %copy.23 = f32[256,896]{0,1:T(8,128)} copy(f32[256,896]{1,0:T(8,128)} %convolution_add_fusion) | data formatting | bytes 1835008 | tf_op jit(solution)/shard_map/add | solution.py:57
  18.3 2.2 %reshape.119 = f32[1792,128]{1,0:T(8,128)} reshape(f32[256,896]{1,0:T(8,128)} %convolution_add_fusion) | data formatting | bytes 1835008 | tf_op jit(solution)/shard_map/reshape | solution.py:58
  22.2 1.1 fusion.18
  23.5 33.5 %all_gather.6 = bf16[2048,128]{0,1:T(8,128)(2,1)S(1)} all-gather(bf16[256,128]{0,1:T(8,128)(2,1)} %get-tuple-element.38), channel_id=1, replica_groups=mesh['seq'=8,'head'=4] {'seq'}, dimensions={0}, use_global_device_ids=true | all-gather | bytes 589824 | tf_op jit(solution)/shard_map/all_gather | solution.py:89
  57.0 1.9 fusion.10
  58.9 33.4 %all_gather.7 = bf16[2048,128]{1,0:T(8,128)(2,1)} all-gather(bf16[256,128]{1,0:T(8,128)(2,1)S(1)} %fusion.10), channel_id=1, replica_groups=mesh['seq'=8,'head'=4] {'seq'}, dimensions={0}, use_global_device_ids=true | all-gather | bytes 589824 | tf_op jit(solution)/shard_map/all_gather | solution.py:90
  93.6 1.0 concatenate.28
  95.8 1.1 mul.134
  96.8 1.4 copy.25
  98.3 1.0 concatenate.29
  99.3 2.4 %fusion.13 = bf16[1792,128]{1,0:T(8,128)(2,1)S(1)} fusion(f32[1792,128]{1,0:T(8,128)} %mul.134, f32[1792,64]{1,0:T(8,128)} %concatenate.29, f32[1792,64]{1,0:T(8,128)} %concatenate.28, f32[1792,128]{1,0:T(8,128)S(1)} %copy-done.3, f32[1792,128]{1,0:T(8,128)} %mul.131), kind=kLoop, calls=%fused_computation.23 | loop fusion | flops 1376256 | bytes 4128768 | tf_op jit(solution)/shard_map/convert_element_type | solution.py:59
  101.7 22.9 %conditional.1 = (f32[1792]{0:T(1024)S(1)}, f32[1792,128]{1,0:T(8,128)S(1)}) conditional(s32[]{:T(128)} %convert_element_type.49, () %tuple.16, (s32[]{:T(128)}, bf16[1792,128]{1,0:T(8,128)(2,1)S(1)}, bf16[2048,128]{0,1:T(8,128)(2,1)S(1)}, bf16[2048,128]{1,0:T(8,128)(2,1)S(1)}) %tuple.32), branch_computations={%region_1.0_spmd, %region_2.5_spmd} | conditional | flops 1915748608 | bytes 46516244 | solution.py:99
  102.6 7.3 %select_reduce_fusion = (f32[1792]{0:T(1024)S(1)}, f32[1792,2048]{1,0:T(8,128)}) fusion(pred[2048]{0:T(1024)(128)(4,1)S(1)} %iota_compare_fusion, bf16[1792,128]{1,0:T(8,128)(2,1)S(1)} %get-tuple-element.9, bf16[2048,128]{0,1:T(8,128)(2,1)S(1)} %get-tuple-element.28), kind=kOutput, calls=%fused_computation.1 | convolution fusion | flops 946862336 | bytes 15672320 | tf_op jit(solution)/shard_map/cond/branch_1_fun/dot_general | solution.py:32
  109.9 8.2 %fusion.1 = f32[1792]{0:T(1024)S(1)} fusion(f32[1792,2048]{1,0:T(8,128)} %get-tuple-element.31, f32[1792]{0:T(1024)S(1)} %broadcast_maximum_fusion, pred[2048]{0:T(1024)(128)(4,1)S(1)} %iota_compare_fusion), kind=kLoop, calls=%fused_computation.3 | loop fusion | flops 14678272 | bytes 14696448 | tf_op jit(solution)/shard_map/cond/branch_1_fun/reduce_sum | solution.py:79
  118.0 6.6 %fusion.2 = f32[1792,128]{1,0:T(8,128)S(1)} fusion(bf16[2048,128]{1,0:T(8,128)(2,1)S(1)} %get-tuple-element.11, f32[1792,2048]{1,0:T(8,128)} %get-tuple-element.31, f32[1792]{0:T(1024)S(1)} %broadcast_maximum_fusion, pred[2048]{0:T(1024)(128)(4,1)S(1)} %iota_compare_fusion), kind=kOutput, calls=%fused_computation.4 | convolution fusion | flops 954204160 | bytes 16131072 | tf_op jit(solution)/shard_map/cond/branch_1_fun/dot_general | solution.py:80
  125.4 6.1 %convolution_convert_fusion = bf16[256,3584]{1,0:T(8,128)(2,1)} fusion(bf16[256,896]{1,0:T(8,128)(2,1)S(1)} %reshape.122, bf16[896,3584]{1,0:T(8,128)(2,1)} %param.22), kind=kOutput, calls=%fused_computation.10 | convolution fusion | flops 1645084672 | bytes 8716288 | tf_op jit(solution)/shard_map/dot_general | solution.py:103
  131.6 4.0 %copy.29 = bf16[256,3584]{0,1:T(8,128)(2,1)} copy(bf16[256,3584]{1,0:T(8,128)(2,1)} %convolution_convert_fusion) | data formatting | bytes 3670016
  135.6 30.9 %reduce-scatter.4.cloned.1.call-done = bf16[896,256]{1,0:T(8,128)(2,1)} async-done(((bf16[3584,256]{1,0:T(8,128)(2,1)}), bf16[896,256]{1,0:T(8,128)(2,1)}) %reduce-scatter.4.cloned.1.call-update) | async-done | bytes 458768
  166.5 1.3 copy.30
  168.0 5.8 %psum.21 = f32[256]{0:T(256)S(1)} all-reduce(f32[256]{0:T(256)S(1)} %multiply_reduce_fusion), channel_id=1, replica_groups=mesh['seq'=8,'head'=4] {'head'}, use_global_device_ids=true, to_apply=%region_7.8 | all-reduce | flops 256 | bytes 2048 | tf_op jit(solution)/shard_map/psum | solution.py:112
  174.8 21.5 %psum.22 = f32[896]{0:T(1024)S(1)} all-reduce(f32[896]{0:T(1024)S(1)} %get-tuple-element.32), channel_id=1, replica_groups=mesh['seq'=8,'head'=4] {'seq'}, use_global_device_ids=true, to_apply=%region_9.10 | all-reduce | flops 896 | bytes 7168 | tf_op jit(solution)/shard_map/psum | solution.py:116
  196.9 6.3 %psum.23 = f32[]{:T(128)} all-reduce(f32[]{:T(128)} %multiply_reduce_fusion.1), channel_id=1, replica_groups=mesh['seq'=8,'head'=4] {'head'}, use_global_device_ids=true, to_apply=%region_11.12 | all-reduce | flops 1 | bytes 8 | tf_op jit(solution)/shard_map/psum | solution.py:118
  (45 shorter events, 7.6 us)
Async XLA Ops:
  7.2 14.0 %copy-start = (bf16[3584,128]{1,0:T(8,128)(2,1)S(1)}, bf16[3584,128]{1,0:T(8,128)(2,1)}, u32[]{:S(2)}) copy-start(bf16[3584,128]{1,0:T(8,128)(2,1)} %param.18) | copy-start | bytes 2752516
  7.2 159.3 %reduce-scatter.4.cloned.1.call-start = ((), (), s32[]{:S(2)}) async-start(), calls=%async_computation.1 | async-start | bytes 2293760
  15.7 5.4 %copy-start.1 = (bf16[256,3584]{1,0:T(8,128)(2,1)S(1)}, bf16[256,3584]{1,0:T(8,128)(2,1)}, u32[]{:S(2)}) copy-start(bf16[256,3584]{1,0:T(8,128)(2,1)} %param.13) | copy-start | bytes 5505028
  15.7 5.5 %copy-start.7 = (f32[3584]{0:T(1024)S(1)}, f32[3584]{0:T(1024)}, u32[]{:S(2)}) copy-start(f32[3584]{0:T(1024)} %param.15) | copy-start | bytes 43012
  15.7 5.5 %copy-start.8 = (f32[128]{0:T(128)S(1)}, f32[128]{0:T(128)}, u32[]{:S(2)}) copy-start(f32[128]{0:T(128)} %param.19) | copy-start | bytes 1540
  18.3 38.7 %copy-start.9 = (f32[128]{0:T(128)S(1)}, f32[128]{0:T(128)}, u32[]{:S(2)}) copy-start(f32[128]{0:T(128)} %param.21) | copy-start | bytes 1540
  23.5 68.8 %copy-start.4 = (f32[256,896]{0,1:T(8,128)S(1)}, f32[256,896]{0,1:T(8,128)}, u32[]{:S(2)}) copy-start(f32[256,896]{0,1:T(8,128)} %copy.23) | copy-start | bytes 2752516
  95.7 3.6 %copy-start.3 = (f32[1792,128]{1,0:T(8,128)S(1)}, f32[1792,128]{1,0:T(8,128)}, u32[]{:S(2)}) copy-start(f32[1792,128]{1,0:T(8,128)} %reshape.119) | copy-start | bytes 2752516
  99.3 2.4 %copy-start.5 = (bf16[2048,128]{1,0:T(8,128)(2,1)S(1)}, bf16[2048,128]{1,0:T(8,128)(2,1)}, u32[]{:S(2)}) copy-start(bf16[2048,128]{1,0:T(8,128)(2,1)} %all_gather.7) | copy-start | bytes 1572868
  131.6 36.2 %copy-start.2 = (bf16[256,3584]{1,0:T(8,128)(2,1)S(1)}, bf16[256,3584]{1,0:T(8,128)(2,1)}, u32[]{:S(2)}) copy-start(bf16[256,3584]{1,0:T(8,128)(2,1)} %param.13) | copy-start | bytes 5505028
  131.6 42.2 %copy-start.6 = (f32[896]{0:T(1024)S(1)}, f32[896]{0:T(1024)}, u32[]{:S(2)}) copy-start(f32[896]{0:T(1024)} %param.23) | copy-start | bytes 10756
Sparse Core Ops, SparseCore 0:
  135.7 30.7 reduce-scatter.3
where the time goes:
time: 212 us; the launch traced here: 211 us
  blocking collectives  100 us (47%)
  waiting for transfers between devices  30.9 us (15%)
  matrix products  29.3 us (14%)
  other arithmetic  18.1 us (9%)
  local copies, waits for them, and re-layouts  16.8 us (8%)
  between operations  15.6 us (7%)
    all_gather x1, blocking collectives, body(): lax.all_gather(keys, 'seq', axis=0, tiled=True)  33.5 us
    all_gather x1, blocking collectives, body(): lax.all_gather(values, 'seq', axis=0, tiled=True)  33.4 us
    unnamed x2, waiting for transfers between devices  30.9 us
    psum x1, blocking collectives, body(): pooled_sum = lax.psum(local_sum, 'seq')  21.5 us
    reduce_sum x1, other arithmetic, absorb(): total = jnp.sum(weights, axis=1)  8.15 us
    dot_general x1, matrix products, key_scores(): lax.dot_general(queries, key_block, (((1,), (1,)), ((), ())), preferred_e...  7.28 us
    dot_general x1, matrix products, absorb(): jnp.dot(weights.astype(jnp.bfloat16), v_piece, preferred_element_type=jnp...  6.61 us
    dot_general x1, matrix products, body(): jnp.dot(normed, q_weight, preferred_element_type=jnp.float32) + q_bias  6.46 us
  transfers between devices with their start and end apart: 1, of which 1 were waited for; matrix products, arithmetic and copies ran while one was open for 0% of the time, Pallas kernels for 0%

commit v1 on v0

--- a/solution.py
+++ b/solution.py
@@ -113,7 +113,11 @@
     final = hidden_full * lax.rsqrt(squares[:, None] / D + epsilon) * final_gain
     row_live = positions < limit
     local_sum = jnp.sum(jnp.where(row_live[:, None], final, 0.0), axis=0)
-    pooled_sum = lax.psum(local_sum, "seq")
+
+    def start_figure(net_axis, chunk):
+        return jnp.sum(lax.all_gather(chunk, axis_name=net_axis), axis=0)
+
+    pooled_sum = start_figure("seq", local_sum)
     mean = pooled_sum / limit.astype(jnp.float32)
     power = lax.psum(jnp.sum(mean * mean), "head")
     embedding = mean * lax.rsqrt(power / D + epsilon)

time: 212 us -> 221 us (1.042)
  blocking collectives: 100 us -> 110 us
    all_gather x0 -> x1, blocking collectives: none -> 30.8 us  [start_figure(): return jnp.sum(lax.all_gather(chunk, axis_name=net_axis), axis=0)]
    psum x1 -> x0, blocking collectives: 21.5 us -> none  [body(): pooled_sum = lax.psum(local_sum, 'seq')]
    unnamed x22 -> x23, local copies, waits for them, and re-layouts: 5.26 us -> 5.27 us
where the time goes in v1:
time: 221 us
  blocking collectives  110 us (50%)
  waiting for transfers between devices  30.9 us (14%)
  matrix products  29.3 us (13%)
  other arithmetic  18.1 us (8%)
  local copies, waits for them, and re-layouts  16.8 us (8%)
  between operations  15.6 us (7%)
    all_gather x1, blocking collectives, body(): lax.all_gather(keys, 'seq', axis=0, tiled=True)  33.5 us
    all_gather x1, blocking collectives, body(): lax.all_gather(values, 'seq', axis=0, tiled=True)  33.4 us
    unnamed x2, waiting for transfers between devices  30.9 us
    all_gather x1, blocking collectives, start_figure(): return jnp.sum(lax.all_gather(chunk, axis_name=net_axis), axis=0)  30.8 us
    reduce_sum x1, other arithmetic, absorb(): total = jnp.sum(weights, axis=1)  8.15 us
    dot_general x1, matrix products, key_scores(): lax.dot_general(queries, key_block, (((1,), (1,)), ((), ())), preferred_e...  7.28 us
    dot_general x1, matrix products, absorb(): jnp.dot(weights.astype(jnp.bfloat16), v_piece, preferred_element_type=jnp...  6.61 us
    dot_general x1, matrix products, body(): jnp.dot(normed, q_weight, preferred_element_type=jnp.float32) + q_bias  6.46 us
  transfers between devices with their start and end apart: 1, of which 1 were waited for; matrix products, arithmetic and copies ran while one was open for 0% of the time, Pallas kernels for 0%

profile of v1, /device:TPU:0, one launch (start us, length us, event | category | flops | bytes accessed | tf_op | source)
XLA Modules:
  0.0 220.7 jit_solution(11962654678633053908)
XLA Ops:
  7.2 2.0 fusion.7
  9.3 6.5 %convolution_add_fusion = f32[256,896]{1,0:T(8,128)} fusion(bf16[3584,896]{1,0:T(8,128)(2,1)} %param.16, f32[896]{0:T(1024)} %param.17, bf16[256,3584]{1,0:T(8,128)(2,1)} %param.13, f32[3584]{0:T(1024)} %param.15, f32[256]{0:T(256)S(1)} %add_rsqrt_fusion.1), kind=kOutput, calls=%fused_computation.16 | convolution fusion | flops 1648066560 | bytes 9193984 | tf_op jit(solution)/shard_map/dot_general | solution.py:57
  15.7 2.6 %copy.23 = f32[256,896]{0,1:T(8,128)} copy(f32[256,896]{1,0:T(8,128)} %convolution_add_fusion) | data formatting | bytes 1835008 | tf_op jit(solution)/shard_map/add | solution.py:57
  18.3 2.2 reshape.119
  22.2 1.1 fusion.18
  23.5 33.5 %all_gather.12 = bf16[2048,128]{0,1:T(8,128)(2,1)S(1)} all-gather(bf16[256,128]{0,1:T(8,128)(2,1)} %get-tuple-element.38), channel_id=1, replica_groups=mesh['seq'=8,'head'=4] {'seq'}, dimensions={0}, use_global_device_ids=true | all-gather | bytes 589824 | tf_op jit(solution)/shard_map/all_gather | solution.py:89
  57.0 1.9 fusion.10
  58.9 33.4 %all_gather.13 = bf16[2048,128]{1,0:T(8,128)(2,1)} all-gather(bf16[256,128]{1,0:T(8,128)(2,1)S(1)} %fusion.10), channel_id=1, replica_groups=mesh['seq'=8,'head'=4] {'seq'}, dimensions={0}, use_global_device_ids=true | all-gather | bytes 589824 | tf_op jit(solution)/shard_map/all_gather | solution.py:90
  93.6 1.0 concatenate.28
  95.8 1.1 mul.134
  96.8 1.4 copy.25
  98.3 1.0 concatenate.29
  99.3 2.4 %fusion.13 = bf16[1792,128]{1,0:T(8,128)(2,1)S(1)} fusion(f32[1792,128]{1,0:T(8,128)} %mul.134, f32[1792,64]{1,0:T(8,128)} %concatenate.29, f32[1792,64]{1,0:T(8,128)} %concatenate.28, f32[1792,128]{1,0:T(8,128)S(1)} %copy-done.3, f32[1792,128]{1,0:T(8,128)} %mul.131), kind=kLoop, calls=%fused_computation.23 | loop fusion | flops 1376256 | bytes 4128768 | tf_op jit(solution)/shard_map/convert_element_type | solution.py:59
  101.7 22.9 %conditional.1 = (f32[1792]{0:T(1024)S(1)}, f32[1792,128]{1,0:T(8,128)S(1)}) conditional(s32[]{:T(128)} %convert_element_type.49, () %tuple.16, (s32[]{:T(128)}, bf16[1792,128]{1,0:T(8,128)(2,1)S(1)}, bf16[2048,128]{0,1:T(8,128)(2,1)S(1)}, bf16[2048,128]{1,0:T(8,128)(2,1)S(1)}) %tuple.32), branch_computations={%region_1.0_spmd, %region_2.5_spmd} | conditional | flops 1915748608 | bytes 46516244 | solution.py:99
  102.6 7.3 %select_reduce_fusion = (f32[1792]{0:T(1024)S(1)}, f32[1792,2048]{1,0:T(8,128)}) fusion(pred[2048]{0:T(1024)(128)(4,1)S(1)} %iota_compare_fusion, bf16[1792,128]{1,0:T(8,128)(2,1)S(1)} %get-tuple-element.9, bf16[2048,128]{0,1:T(8,128)(2,1)S(1)} %get-tuple-element.28), kind=kOutput, calls=%fused_computation.1 | convolution fusion | flops 946862336 | bytes 15672320 | tf_op jit(solution)/shard_map/cond/branch_1_fun/dot_general | solution.py:32
  109.9 8.2 %fusion.1 = f32[1792]{0:T(1024)S(1)} fusion(f32[1792,2048]{1,0:T(8,128)} %get-tuple-element.31, f32[1792]{0:T(1024)S(1)} %broadcast_maximum_fusion, pred[2048]{0:T(1024)(128)(4,1)S(1)} %iota_compare_fusion), kind=kLoop, calls=%fused_computation.3 | loop fusion | flops 14678272 | bytes 14696448 | tf_op jit(solution)/shard_map/cond/branch_1_fun/reduce_sum | solution.py:79
  118.0 6.6 %fusion.2 = f32[1792,128]{1,0:T(8,128)S(1)} fusion(bf16[2048,128]{1,0:T(8,128)(2,1)S(1)} %get-tuple-element.11, f32[1792,2048]{1,0:T(8,128)} %get-tuple-element.31, f32[1792]{0:T(1024)S(1)} %broadcast_maximum_fusion, pred[2048]{0:T(1024)(128)(4,1)S(1)} %iota_compare_fusion), kind=kOutput, calls=%fused_computation.4 | convolution fusion | flops 954204160 | bytes 16131072 | tf_op jit(solution)/shard_map/cond/branch_1_fun/dot_general | solution.py:80
  125.4 6.1 %convolution_convert_fusion = bf16[256,3584]{1,0:T(8,128)(2,1)} fusion(bf16[256,896]{1,0:T(8,128)(2,1)S(1)} %reshape.122, bf16[896,3584]{1,0:T(8,128)(2,1)} %param.22), kind=kOutput, calls=%fused_computation.10 | convolution fusion | flops 1645084672 | bytes 8716288 | tf_op jit(solution)/shard_map/dot_general | solution.py:103
  131.6 4.0 %copy.29 = bf16[256,3584]{0,1:T(8,128)(2,1)} copy(bf16[256,3584]{1,0:T(8,128)(2,1)} %convolution_convert_fusion) | data formatting | bytes 3670016
  135.6 30.9 %reduce-scatter.4.cloned.1.call-done = bf16[896,256]{1,0:T(8,128)(2,1)} async-done(((bf16[3584,256]{1,0:T(8,128)(2,1)}), bf16[896,256]{1,0:T(8,128)(2,1)}) %reduce-scatter.4.cloned.1.call-update) | async-done | bytes 458768
  166.5 1.3 copy.30
  168.0 5.8 %psum.14 = f32[256]{0:T(256)S(1)} all-reduce(f32[256]{0:T(256)S(1)} %multiply_reduce_fusion), channel_id=1, replica_groups=mesh['seq'=8,'head'=4] {'head'}, use_global_device_ids=true, to_apply=%region_7.8 | all-reduce | flops 256 | bytes 2048 | tf_op jit(solution)/shard_map/psum | solution.py:112
  174.8 30.8 %all-gather.1 = f32[8,1,896]{2,1,0:T(1,128)S(1)} all-gather(f32[1,1,896]{2,1,0:T(1,128)S(1)} %reshape.124), channel_id=2, replica_groups=mesh['seq'=8,'head'=4] {'seq'}, dimensions={0}, use_global_device_ids=true | all-gather | bytes 32256 | tf_op jit(solution)/shard_map/all_gather | solution.py:118
  206.3 6.3 %psum.15 = f32[]{:T(128)} all-reduce(f32[]{:T(128)} %multiply_reduce_fusion.1), channel_id=1, replica_groups=mesh['seq'=8,'head'=4] {'head'}, use_global_device_ids=true, to_apply=%region_11.12 | all-reduce | flops 1 | bytes 8 | tf_op jit(solution)/shard_map/psum | solution.py:122
  (47 shorter events, 7.6 us)
Async XLA Ops:
  7.2 14.0 %copy-start = (bf16[3584,128]{1,0:T(8,128)(2,1)S(1)}, bf16[3584,128]{1,0:T(8,128)(2,1)}, u32[]{:S(2)}) copy-start(bf16[3584,128]{1,0:T(8,128)(2,1)} %param.18) | copy-start | bytes 2752516
  7.2 159.3 %reduce-scatter.4.cloned.1.call-start = ((), (), s32[]{:S(2)}) async-start(), calls=%async_computation.1 | async-start | bytes 2293760
  15.7 5.4 %copy-start.1 = (bf16[256,3584]{1,0:T(8,128)(2,1)S(1)}, bf16[256,3584]{1,0:T(8,128)(2,1)}, u32[]{:S(2)}) copy-start(bf16[256,3584]{1,0:T(8,128)(2,1)} %param.13) | copy-start | bytes 5505028
  15.7 5.5 %copy-start.7 = (f32[3584]{0:T(1024)S(1)}, f32[3584]{0:T(1024)}, u32[]{:S(2)}) copy-start(f32[3584]{0:T(1024)} %param.15) | copy-start | bytes 43012
  15.7 5.5 %copy-start.8 = (f32[128]{0:T(128)S(1)}, f32[128]{0:T(128)}, u32[]{:S(2)}) copy-start(f32[128]{0:T(128)} %param.19) | copy-start | bytes 1540
  18.3 38.7 %copy-start.9 = (f32[128]{0:T(128)S(1)}, f32[128]{0:T(128)}, u32[]{:S(2)}) copy-start(f32[128]{0:T(128)} %param.21) | copy-start | bytes 1540
  23.5 68.8 %copy-start.4 = (f32[256,896]{0,1:T(8,128)S(1)}, f32[256,896]{0,1:T(8,128)}, u32[]{:S(2)}) copy-start(f32[256,896]{0,1:T(8,128)} %copy.23) | copy-start | bytes 2752516
  95.7 3.6 %copy-start.3 = (f32[1792,128]{1,0:T(8,128)S(1)}, f32[1792,128]{1,0:T(8,128)}, u32[]{:S(2)}) copy-start(f32[1792,128]{1,0:T(8,128)} %reshape.119) | copy-start | bytes 2752516
  99.3 2.4 %copy-start.5 = (bf16[2048,128]{1,0:T(8,128)(2,1)S(1)}, bf16[2048,128]{1,0:T(8,128)(2,1)}, u32[]{:S(2)}) copy-start(bf16[2048,128]{1,0:T(8,128)(2,1)} %all_gather.13) | copy-start | bytes 1572868
  131.6 36.2 %copy-start.2 = (bf16[256,3584]{1,0:T(8,128)(2,1)S(1)}, bf16[256,3584]{1,0:T(8,128)(2,1)}, u32[]{:S(2)}) copy-start(bf16[256,3584]{1,0:T(8,128)(2,1)} %param.13) | copy-start | bytes 5505028
  131.6 42.2 %copy-start.6 = (f32[896]{0:T(1024)S(1)}, f32[896]{0:T(1024)}, u32[]{:S(2)}) copy-start(f32[896]{0:T(1024)} %param.23) | copy-start | bytes 10756
Sparse Core Ops, SparseCore 0:
  135.7 30.7 reduce-scatter.3
